TPU v7x, 32 devices: a whole 2x2x4 slice. The times are simulated.
32 devices in a mesh: sweep: 2 (over y), seq: 8 (over z, x), head: 2 (over core).
Axes of the slice: x: 2, y: 2, z: 4, core: 2. Of those that a mesh axis runs over, the one named last changes fastest.
Arguments:
- queries: bfloat16 [2048, 1024], P(('sweep', 'seq'), 'head'), parts along dimension 0, may hold values from -6 to 6
- key_matrix: bfloat16 [2048, 256], P(('sweep', 'seq'), 'head'), parts along dimension 0, may hold values from -6 to 6
- value_matrix: bfloat16 [2048, 256], P(('sweep', 'seq'), 'head'), parts along dimension 0, may hold values from -6 to 6
- segment_ids: int32 [2048], P(('sweep', 'seq')), parts along dimension 0, may hold values from 0 to 16, as said below
Outputs:
- attended: bfloat16 [2048, 1024], P(('sweep', 'seq'), 'head'), parts along dimension 0
There are 2 independent parts, one for each index of `sweep`. A program takes and returns all parts, laid end to end along the dimension named above; each array names one. Nothing has to cross between parts.
Inputs may be any that keep to these rules, and one draw needn't show every extreme that they name: `segment_ids`: never falling. Segment 0 is a prompt at the start of 128 to 256 tokens; each id of 1 to 16 is one response of one or more tokens.
All inputs are finite; a program needn't handle non-finite values.
Results may differ from a plain program's by a relative error of at most 0.005.
Values may be sent and summed in bfloat16 or wider, within the bound.
A program may use at most 64 MiB of HBM per device.

v0:
```python
import math

import jax
import jax.numpy as jnp
from jax import lax
from jax.sharding import PartitionSpec as P

HEAD_WIDTH = 64


NEG_FILL = -1e30


def attend_block(state, query_heads, query_pos, query_seg, key_blk, value_blk, seg_blk, key_start):
    run_max, weight_total, totals = state
    groups = query_heads.shape[1]
    head_size = query_heads.shape[3]
    count = key_blk.shape[0]
    key_pos = key_start + jnp.arange(count, dtype=jnp.int32)
    visible = (key_pos[None, :] <= query_pos[:, None]) & (
        (seg_blk[None, :] == query_seg[:, None]) | (seg_blk[None, :] == 0)
    )

    def update(unused):
        logit_scores = jnp.einsum(
            "opez,hpz->peoh",
            query_heads,
            key_blk.reshape(count, groups, head_size),
            preferred_element_type=jnp.float32,
        ) * (1.0 / math.sqrt(head_size))
        logit_scores = jnp.where(visible, logit_scores, NEG_FILL)
        new_max = jnp.maximum(run_max, jnp.max(logit_scores, axis=-1))
        weights = jnp.where(visible, jnp.exp(logit_scores - new_max[..., None]), 0.0)
        rescale = jnp.exp(run_max - new_max)
        new_sum = weight_total * rescale + jnp.sum(weights, axis=-1)
        mixed_output = jnp.einsum(
            "omhy,yoc->omhc",
            weights.astype(jnp.bfloat16),
            value_blk.reshape(count, groups, head_size),
            preferred_element_type=jnp.float32,
        )
        return (new_max, new_sum, totals * rescale[..., None] + mixed_output)

    def keep(unused):
        return state

    return lax.cond(jnp.any(visible), update, keep, 0)


def build_fold(query_sets):

    def apply_all(states, key_piece, value_piece, seg_piece, start):
        return tuple(
            (
                attend_block(
                    states[number],
                    entry[0],
                    entry[1],
                    entry[2],
                    key_piece,
                    value_piece,
                    seg_piece,
                    start,
                )
                for number, entry in enumerate(query_sets)
            )
        )

    def fold(states, piece, start):
        key_piece, value_piece, seg_piece = piece
        rows = key_piece.shape[0]
        width = 512

        def loop_step(index, carried):
            offset = index * width
            return apply_all(
                carried,
                lax.dynamic_slice_in_dim(key_piece, offset, width, 0),
                lax.dynamic_slice_in_dim(value_piece, offset, width, 0),
                lax.dynamic_slice_in_dim(seg_piece, offset, width, 0),
                offset,
            )

        return lax.fori_loop(0, rows // width, loop_step, states)

    return fold


def start_state(query_heads):
    tok_rows, groups, repeat_factor, head_size = query_heads.shape
    return (
        jnp.full((groups, repeat_factor, tok_rows), NEG_FILL, jnp.float32),
        jnp.zeros((groups, repeat_factor, tok_rows), jnp.float32),
        jnp.zeros((groups, repeat_factor, tok_rows, head_size), jnp.float32),
    )


def finish(state):
    run_max, weight_total, totals = state
    result = totals / weight_total[..., None]
    groups, repeat_factor, tok_rows, head_size = result.shape
    return (
        jnp.transpose(result, (2, 0, 1, 3))
        .reshape(tok_rows, groups * repeat_factor * head_size)
        .astype(jnp.bfloat16)
    )


def per_device(queries, key_matrix, value_matrix, segment_ids):
    head_size = HEAD_WIDTH
    block_rows = segment_ids.shape[0]
    groups = key_matrix.shape[1] // head_size
    repeat_factor = queries.shape[1] // head_size // groups
    position = lax.axis_index("seq")
    query_pos = position * block_rows + jnp.arange(block_rows, dtype=jnp.int32)
    query_sets = (
        (queries.reshape(block_rows, groups, repeat_factor, head_size), query_pos, segment_ids),
    )
    fold = build_fold(query_sets)
    states = tuple((start_state(entry[0]) for entry in query_sets))
    states = fold(
        states,
        (
            lax.all_gather(key_matrix, "seq", axis=0, tiled=True),
            lax.all_gather(value_matrix, "seq", axis=0, tiled=True),
            lax.all_gather(segment_ids, "seq", axis=0, tiled=True),
        ),
        jnp.int32(0),
    )
    return finish(states[0])


def solution(mesh):
    in_specs = (
        P(("sweep", "seq"), "head"),
        P(("sweep", "seq"), "head"),
        P(("sweep", "seq"), "head"),
        P(("sweep", "seq")),
    )
    out_specs = P(("sweep", "seq"), "head")
    return jax.shard_map(
        per_device, mesh=mesh, in_specs=in_specs, out_specs=out_specs, check_vma=False
    )
```

profile of v0, /device:TPU:0, one launch (start us, length us, event | category | flops | bytes accessed | tf_op | source)
XLA Modules:
  0.0 85.6 jit_solution(3842779649709735597)
XLA Ops:
  0.0 22.4 %all-gather = s32[8,1,128]{2,1,0:T(1,128)S(1)} all-gather(s32[1,1,128]{2,1,0:T(1,128)} %bitcast.47), channel_id=1, replica_groups=mesh['sweep'=2,'seq'=8,'head'=2] {'seq'}, dimensions={0}, use_global_device_ids=true | all-gather | bytes 4608 | tf_op jit(solution)/shard_map/all_gather | solution.py:126
  22.4 0.9 %copy.16 = bf16[128,128]{0,1:T(8,128)(2,1)S(1)} copy(bf16[128,128]{1,0:T(8,128)(2,1)} %param.9) | data formatting | bytes 65536 | tf_op args[1]
  23.3 0.9 %copy.18 = bf16[128,128]{0,1:T(8,128)(2,1)S(1)} copy(bf16[128,128]{1,0:T(8,128)(2,1)} %param.10) | data formatting | bytes 65536 | tf_op args[2]
  24.2 1.0 %copy.17 = bf16[128,512]{0,1:T(8,128)(2,1)S(1)} copy(bf16[128,512]{1,0:T(8,128)(2,1)} %param.8) | data formatting | bytes 262144 | tf_op args[0]
  25.2 26.7 %all_gather.11 = bf16[1024,128]{0,1:T(8,128)(2,1)S(1)} all-gather(bf16[128,128]{0,1:T(8,128)(2,1)S(1)} %copy.18), channel_id=1, replica_groups=mesh['sweep'=2,'seq'=8,'head'=2] {'seq'}, dimensions={0}, use_global_device_ids=true | all-gather | bytes 294912 | tf_op jit(solution)/shard_map/all_gather | solution.py:125
  51.9 26.4 %all_gather.10 = bf16[1024,128]{0,1:T(8,128)(2,1)S(1)} all-gather(bf16[128,128]{0,1:T(8,128)(2,1)S(1)} %copy.16), channel_id=1, replica_groups=mesh['sweep'=2,'seq'=8,'head'=2] {'seq'}, dimensions={0}, use_global_device_ids=true | all-gather | bytes 294912 | tf_op jit(solution)/shard_map/all_gather | solution.py:124
  78.4 6.5 %while.18 = (s32[]{:T(128)}, f32[2,4,128]{2,1,0:T(4,128)S(1)}, f32[2,4,128]{2,1,0:T(4,128)S(1)}, f32[2,4,128,64]{2,3,1,0:T(8,128)S(1)}, s32[1024]{0:T(1024)S(1)}...) while((s32[]{:T(128)}, f32[2,4,128]{2,1,0:T(4,128)S(1)}, ...), condition=%wide.region_6.7_spmd.clone, body=%wide.region_0.6_spmd.clone.sunk | while | flops 141495424 | bytes 8074049 | solution.py:84
  78.4 0.1 broadcast_compare_fusion.2
  78.5 1.6 %fusion.18 = (pred[]{:T(512)}, pred[128,512]{0,1:T(8,128)(4,1)S(1)}) fusion(pred[512]{0:T(512)(128)(4,1)S(1)} %get-tuple-element.383, s32[128]{0:T(128)} %get-tuple-element.429, s32[512]{0:T(512)S(1)} %get-tuple-element.384, s32[128]{0:T(128)S(1)} %iota_add_fusion.4, s32[512]{0:T(512)S(1)} %iota_add_fusion.5), kind=kLoop, calls=%fused_computation.23.clone.1 | loop fusion | flops 327679 | bytes 71169 | tf_op jit(solution)/shard_map/while/body/eval_jaxpr/reduce_or | solution.py:47
  80.7 1.8 %conditional.3 = ((f32[2,4,128]{2,1,0:T(4,128)S(1)}, f32[2,4,128]{2,1,0:T(4,128)S(1)}, f32[2,4,128,64]{2,3,1,0:T(8,128)S(1)})) conditional(s32[]{:T(128)} %convert_element_type.29, (f32[2,4,128]{2,1,0:T(4,128)S(1)}, f32[2,4,128]{2,1,0:T(4,128)S(1)}, f32[2,4,128,64]{2,3,1,0:T(8,128)S(1)}) %tuple.56, (pred[128,512]{0,1:T(8,128)(4,1)S(1)}, ...), branch_computations={%region_2.0_spmd, %region_3.5_spmd} | conditional | flops 141166592 | bytes 7995428 | solution.py:47
  80.8 0.5 fusion.2
  81.3 0.5 fusion.4
  81.8 0.6 convolution_add_fusion
  82.5 0.1 broadcast_compare_fusion.2
  82.6 1.6 %fusion.18 = (pred[]{:T(512)}, pred[128,512]{0,1:T(8,128)(4,1)S(1)}) fusion(pred[512]{0:T(512)(128)(4,1)S(1)} %get-tuple-element.383, s32[128]{0:T(128)} %get-tuple-element.429, s32[512]{0:T(512)S(1)} %get-tuple-element.384, s32[128]{0:T(128)S(1)} %iota_add_fusion.4, s32[512]{0:T(512)S(1)} %iota_add_fusion.5), kind=kLoop, calls=%fused_computation.23.clone.1 | loop fusion | flops 327679 | bytes 71169 | tf_op jit(solution)/shard_map/while/body/eval_jaxpr/reduce_or | solution.py:47
  84.9 0.8 copy.19
  (13 shorter events, 0.1 us)
where the time goes:
time: 86 us; the launch traced here: 85.6 us
  blocking collectives  75.6 us (88%)
  other arithmetic  3.92 us (5%)
  local copies, waits for them, and re-layouts  3.59 us (4%)
  loops' own time  1.39 us (2%)
  matrix products  1.15 us (1%)
    all_gather x1, blocking collectives, per_device(): lax.all_gather(value_matrix, 'seq', axis=0, tiled=True)  26.7 us
    all_gather x1, blocking collectives, per_device(): lax.all_gather(key_matrix, 'seq', axis=0, tiled=True)  26.4 us
    all_gather x1, blocking collectives, per_device(): lax.all_gather(segment_ids, 'seq', axis=0, tiled=True)  22.4 us
    reduce_or x2, other arithmetic, attend_block(): return lax.cond(jnp.any(visible), update, keep, 0)  3.19 us
    unnamed x3, local copies, waits for them, and re-layouts  2.76 us

commit v1 on v0

v1 whole, which is shorter than its diff:
```python
import functools
import math

import jax
import jax.numpy as jnp
from jax import lax
from jax.experimental import pallas as pl
from jax.experimental.pallas import tpu as pltpu
from jax.sharding import PartitionSpec as P

HEAD_WIDTH = 64
NEG_FILL = -1e30
MESH = pl.DeviceIdType.MESH


def kernel(n, inner, q_hbm, k_hbm, v_hbm, s_hbm, o_ref, qv, kbuf, vbuf, sbuf, qm, run_max, acc,
           in_sem, col_sem, row_sem, recv_sem):
    rows = k_hbm.shape[0]
    width = k_hbm.shape[1]
    half = HEAD_WIDTH
    groups = width // half
    tiles = q_hbm.shape[1] // width
    per_group = tiles // groups
    outer = n // inner
    me = lax.axis_index("seq")
    z = me // inner
    x = me % inner
    partner = z * inner + (inner - 1 - x)
    bufs = (sbuf, kbuf, vbuf)

    loads = [
        pltpu.make_async_copy(src, dst, in_sem.at[i])
        for i, (src, dst) in enumerate(
            ((s_hbm, sbuf.at[me]), (k_hbm, kbuf.at[me]), (v_hbm, vbuf.at[me]), (q_hbm, qv))
        )
    ]
    for load in loads:
        load.start()

    barrier = pltpu.get_barrier_semaphore()

    def greet(i, c):
        other = (z + 1 + i) % outer
        pl.semaphore_signal(barrier, inc=1, device_id={"seq": other * inner + x}, device_id_type=MESH)
        return c

    if inner == 2:
        pl.semaphore_signal(barrier, inc=1, device_id={"seq": partner}, device_id_type=MESH)
    lax.fori_loop(0, outer - 1, greet, 0)
    pl.semaphore_wait(barrier, outer - 1 + inner - 1)

    def along_column(kind, target):
        return pltpu.make_async_remote_copy(
            src_ref=bufs[kind].at[me], dst_ref=bufs[kind].at[me],
            send_sem=col_sem.at[kind, target], recv_sem=recv_sem.at[kind, me],
            device_id={"seq": target * inner + x}, device_id_type=MESH)

    def across(kind, row):
        block = row * inner + x
        return pltpu.make_async_remote_copy(
            src_ref=bufs[kind].at[block], dst_ref=bufs[kind].at[block],
            send_sem=row_sem.at[kind, row], recv_sem=recv_sem.at[kind, block],
            device_id={"seq": partner}, device_id_type=MESH)

    def arrival(kind, block):
        return pltpu.make_async_remote_copy(
            src_ref=bufs[kind].at[block], dst_ref=bufs[kind].at[block],
            send_sem=col_sem.at[kind, z], recv_sem=recv_sem.at[kind, block],
            device_id={"seq": partner}, device_id_type=MESH)

    for load in loads[:3]:
        load.wait()
    if inner == 2:
        @pl.when(x == 0)
        def _():
            for kind in range(3):
                across(kind, z).start()

    def send_column(i, c):
        for kind in range(3):
            along_column(kind, outer - 1 - i).start()
        return c

    lax.fori_loop(0, outer - 1 - z, send_column, 0)
    loads[3].wait()

    scale = 1.0 / math.sqrt(half)
    zeros = jnp.zeros((rows, half), jnp.bfloat16)
    for g in range(groups):
        for i in range(per_group):
            at = (g * per_group + i) * width
            lo = (qv[:, at:at + half] * scale).astype(jnp.bfloat16)
            hi = (qv[:, at + half:at + width] * scale).astype(jnp.bfloat16)
            qm[g, i] = jnp.concatenate([lo, zeros], axis=1)
            qm[g, per_group + i] = jnp.concatenate([zeros, hi], axis=1)

    seg_q = jnp.transpose(jnp.broadcast_to(sbuf[me], (rows, rows)))

    def attend(kk, vv, vis, first):
        count = kk.shape[0]
        bias = jnp.where(vis, 0.0, NEG_FILL).astype(jnp.float32)
        ones = jnp.ones((count, half), jnp.bfloat16)
        for g in range(groups):
            kg = kk[:, g * half:(g + 1) * half]
            vg = vv[:, g * half:(g + 1) * half]
            kd = jnp.concatenate([kg, kg], axis=1)
            heads = 2 * per_group
            s = lax.dot_general(
                qm[g].reshape(heads * rows, width), kd, (((1,), (1,)), ((), ())),
                preferred_element_type=jnp.float32)
            s = s.reshape(heads, rows, count) + bias[None]
            top = jnp.max(s, axis=-1, keepdims=True)
            if first:
                new = jnp.broadcast_to(top, (heads, rows, rows))
            else:
                old = run_max[g]
                new = jnp.maximum(old, top)
            run_max[g] = new
            p = jnp.exp(s - jnp.concatenate([new] * (count // rows), axis=-1)).astype(jnp.bfloat16)
            sides = (jnp.concatenate([vg, ones], axis=1), jnp.concatenate([ones, vg], axis=1))
            for side in range(2):
                part = slice(side * per_group, (side + 1) * per_group)
                mixed = jnp.dot(
                    p[part].reshape(per_group * rows, count), sides[side],
                    preferred_element_type=jnp.float32).reshape(per_group, rows, width)
                if first:
                    acc[g, part] = mixed
                else:
                    acc[g, part] = acc[g, part] * jnp.exp(old[part] - new[part]) + mixed

    row_at = lax.broadcasted_iota(jnp.int32, (rows, rows), 0)
    col_at = lax.broadcasted_iota(jnp.int32, (rows, rows), 1)
    seg_k = jnp.broadcast_to(sbuf[me], (rows, rows))
    attend(kbuf[me], vbuf[me], (col_at <= row_at) & ((seg_k == seg_q) | (seg_k == 0)), True)

    def seen(seg):
        seg = jnp.broadcast_to(seg, (rows, rows))
        return (seg == seg_q) | (seg == 0)

    def take(row):
        for kind in range(3):
            arrival(kind, row * inner + x).wait_recv()
            if inner == 2:
                across(kind, row).start()

    @pl.when(z > 0)
    def _():
        take(z - 1)

    if inner == 2:
        @pl.when(x == 1)
        def _():
            for kind in range(3):
                arrival(kind, partner).wait_recv()
            attend(kbuf[partner], vbuf[partner], seen(sbuf[partner]), False)

    def step(i, c):
        row = z - 1 - i

        @pl.when(row > 0)
        def _():
            take(row - 1)

        if inner == 2:
            for kind in range(3):
                arrival(kind, row * inner + 1 - x).wait_recv()
        first = row * inner
        kk = kbuf[pl.ds(first, inner)].reshape(inner * rows, width)
        vv = vbuf[pl.ds(first, inner)].reshape(inner * rows, width)
        vis = jnp.concatenate(
            [jnp.where(seen(sbuf[first + i]), 1, 0) for i in range(inner)], axis=1) == 1
        attend(kk, vv, vis, False)
        return c

    lax.fori_loop(0, z, step, 0)

    left = lax.broadcasted_iota(jnp.int32, (rows, width), 1) < half
    for g in range(groups):
        for i in range(per_group):
            a = acc[g, i]
            b = acc[g, per_group + i]
            total = pltpu.roll(jnp.where(left, b, a), half, 1)
            at = (g * per_group + i) * width
            o_ref[:, at:at + width] = (jnp.where(left, a, b) / total).astype(o_ref.dtype)

    if inner == 2:
        @pl.when(x == 0)
        def _():
            for kind in range(3):
                across(kind, z).wait_send()

        def drain_row(row, c):
            for kind in range(3):
                across(kind, row).wait_send()
            return c

        lax.fori_loop(0, z, drain_row, 0)

    def drain_column(i, c):
        for kind in range(3):
            along_column(kind, outer - 1 - i).wait_send()
        return c

    lax.fori_loop(0, outer - 1 - z, drain_column, 0)


def per_device(n, queries, key_matrix, value_matrix, segment_ids):
    rows, width = key_matrix.shape
    inner = 2 if n % 2 == 0 else 1
    groups = width // HEAD_WIDTH
    heads = queries.shape[1] // HEAD_WIDTH // groups
    return pl.pallas_call(
        functools.partial(kernel, n, inner),
        out_shape=jax.ShapeDtypeStruct(queries.shape, jnp.bfloat16),
        in_specs=[pl.BlockSpec(memory_space=pl.ANY)] * 4,
        out_specs=pl.BlockSpec(memory_space=pltpu.VMEM),
        scratch_shapes=[
            pltpu.VMEM(queries.shape, jnp.bfloat16),
            pltpu.VMEM((n, rows, width), jnp.bfloat16),
            pltpu.VMEM((n, rows, width), jnp.bfloat16),
            pltpu.VMEM((n, 1, rows), jnp.int32),
            pltpu.VMEM((groups, heads, rows, width), jnp.bfloat16),
            pltpu.VMEM((groups, heads, rows, rows), jnp.float32),
            pltpu.VMEM((groups, heads, rows, width), jnp.float32),
            pltpu.SemaphoreType.DMA((4,)),
            pltpu.SemaphoreType.DMA((3, n // inner)),
            pltpu.SemaphoreType.DMA((3, n // inner)),
            pltpu.SemaphoreType.DMA((3, n)),
        ],
        compiler_params=pltpu.CompilerParams(collective_id=0, has_side_effects=True),
    )(queries, key_matrix, value_matrix, segment_ids.reshape(1, rows))


def solution(mesh):
    blocks = P(("sweep", "seq"), "head")
    return jax.shard_map(
        functools.partial(per_device, mesh.shape["seq"]),
        mesh=mesh,
        in_specs=(blocks, blocks, blocks, P(("sweep", "seq"))),
        out_specs=blocks,
        check_vma=False,
    )
```

time: 86 us -> 17.6 us (0.20)
  the two profiles are of different devices: /device:TPU:0 before, /device:TPU:16 now
where the time goes in v1:
time: 17.6 us; the launch traced here: 17.4 us
  Pallas kernels  15.9 us (90%)
  local copies, waits for them, and re-layouts  1.57 us (9%)
    pallas_call x1, Pallas kernels, per_device(): pl.pallas_call(functools.partial(kernel, n, inner), out_shape=jax.ShapeDt...  15.9 us
    unnamed x1, local copies, waits for them, and re-layouts  1.57 us

profile of v1, /device:TPU:16, one launch (start us, length us, event | category | flops | bytes accessed | tf_op | source)
XLA Modules:
  0.0 17.4 jit_solution(3880931855234403203)
XLA Ops:
  0.0 15.9 %shard_map.46 = bf16[128,512]{1,0:T(8,128)(2,1)} custom-call(bf16[128,512]{1,0:T(8,128)(2,1)} %q_hbm.1, bf16[128,128]{1,0:T(8,128)(2,1)} %k_hbm.1, bf16[128,128]{1,0:T(8,128)(2,1)} %v_hbm.1, s32[1,128]{1,0:T(1,128)} %bitcast.1), custom_call_target="tpu_custom_call" | custom-call | tf_op jit(solution)/shard_map/pallas_call | solution.py:212
  15.9 1.6 %copy.6 = bf16[128,512]{1,0:T(8,128)(2,1)} copy(bf16[128,512]{1,0:T(8,128)(2,1)} %shard_map.46) | data formatting | bytes 262144

commit v2 on v1

--- a/solution.py
+++ b/solution.py
@@ -39,21 +39,21 @@
 
     barrier = pltpu.get_barrier_semaphore()
 
-    def greet(i, c):
-        other = (z + 1 + i) % outer
-        pl.semaphore_signal(barrier, inc=1, device_id={"seq": other * inner + x}, device_id_type=MESH)
-        return c
-
     if inner == 2:
         pl.semaphore_signal(barrier, inc=1, device_id={"seq": partner}, device_id_type=MESH)
-    lax.fori_loop(0, outer - 1, greet, 0)
-    pl.semaphore_wait(barrier, outer - 1 + inner - 1)
-
-    def along_column(kind, target):
+
+    @pl.when(z > 0)
+    def _():
+        pl.semaphore_signal(barrier, inc=1, device_id={"seq": me - inner}, device_id_type=MESH)
+
+    pl.semaphore_wait(barrier, inner - 1 + jnp.where(z < outer - 1, 1, 0))
+
+    def onward(kind, row):
+        block = row * inner + x
         return pltpu.make_async_remote_copy(
-            src_ref=bufs[kind].at[me], dst_ref=bufs[kind].at[me],
-            send_sem=col_sem.at[kind, target], recv_sem=recv_sem.at[kind, me],
-            device_id={"seq": target * inner + x}, device_id_type=MESH)
+            src_ref=bufs[kind].at[block], dst_ref=bufs[kind].at[block],
+            send_sem=col_sem.at[kind, row], recv_sem=recv_sem.at[kind, block],
+            device_id={"seq": me + inner}, device_id_type=MESH)
 
     def across(kind, row):
         block = row * inner + x
@@ -65,23 +65,21 @@
     def arrival(kind, block):
         return pltpu.make_async_remote_copy(
             src_ref=bufs[kind].at[block], dst_ref=bufs[kind].at[block],
-            send_sem=col_sem.at[kind, z], recv_sem=recv_sem.at[kind, block],
+            send_sem=in_sem.at[0], recv_sem=recv_sem.at[kind, block],
             device_id={"seq": partner}, device_id_type=MESH)
 
-    for load in loads[:3]:
-        load.wait()
-    if inner == 2:
-        @pl.when(x == 0)
+    for kind in range(3):
+        loads[kind].wait()
+
+        @pl.when(z < outer - 1)
         def _():
-            for kind in range(3):
+            onward(kind, z).start()
+
+        if inner == 2:
+            @pl.when(x == 0)
+            def _():
                 across(kind, z).start()
 
-    def send_column(i, c):
-        for kind in range(3):
-            along_column(kind, outer - 1 - i).start()
-        return c
-
-    lax.fori_loop(0, outer - 1 - z, send_column, 0)
     loads[3].wait()
 
     scale = 1.0 / math.sqrt(half)
@@ -137,15 +135,22 @@
         seg = jnp.broadcast_to(seg, (rows, rows))
         return (seg == seg_q) | (seg == 0)
 
-    def take(row):
+    def take(i, c):
+        row = z - 1 - i
         for kind in range(3):
             arrival(kind, row * inner + x).wait_recv()
+
+            @pl.when(z < outer - 1)
+            def _():
+                onward(kind, row).start()
+
             if inner == 2:
                 across(kind, row).start()
+        return c
 
     @pl.when(z > 0)
     def _():
-        take(z - 1)
+        take(0, 0)
 
     if inner == 2:
         @pl.when(x == 1)
@@ -154,13 +159,10 @@
                 arrival(kind, partner).wait_recv()
             attend(kbuf[partner], vbuf[partner], seen(sbuf[partner]), False)
 
+    lax.fori_loop(1, z, take, 0)
+
     def step(i, c):
         row = z - 1 - i
-
-        @pl.when(row > 0)
-        def _():
-            take(row - 1)
-
         if inner == 2:
             for kind in range(3):
                 arrival(kind, row * inner + 1 - x).wait_recv()
@@ -196,12 +198,14 @@
 
         lax.fori_loop(0, z, drain_row, 0)
 
-    def drain_column(i, c):
-        for kind in range(3):
-            along_column(kind, outer - 1 - i).wait_send()
-        return c
-
-    lax.fori_loop(0, outer - 1 - z, drain_column, 0)
+    @pl.when(z < outer - 1)
+    def _():
+        def drain_column(row, c):
+            for kind in range(3):
+                onward(kind, row).wait_send()
+            return c
+
+        lax.fori_loop(0, z + 1, drain_column, 0)
 
 
 def per_device(n, queries, key_matrix, value_matrix, segment_ids):
@@ -211,7 +215,7 @@
     heads = queries.shape[1] // HEAD_WIDTH // groups
     return pl.pallas_call(
         functools.partial(kernel, n, inner),
-        out_shape=jax.ShapeDtypeStruct(queries.shape, jnp.bfloat16),
+        out_shape=pltpu.VMEM(queries.shape, jnp.bfloat16),
         in_specs=[pl.BlockSpec(memory_space=pl.ANY)] * 4,
         out_specs=pl.BlockSpec(memory_space=pltpu.VMEM),
         scratch_shapes=[

time: 17.6 us -> 14.7 us (0.84)
  the two profiles are of different devices: /device:TPU:16 before, /device:TPU:28 now
where the time goes in v2:
time: 14.7 us; the launch traced here: 14.6 us
  Pallas kernels  13.9 us (95%)
  local copies, waits for them, and re-layouts  0.66 us (4%)
    pallas_call x1, Pallas kernels, per_device(): pl.pallas_call(functools.partial(kernel, n, inner), out_shape=pltpu.VMEM(...  13.9 us
    unnamed x1, local copies, waits for them, and re-layouts  0.66 us

profile of v2, /device:TPU:28, one launch (start us, length us, event | category | flops | bytes accessed | tf_op | source)
XLA Modules:
  0.0 14.6 jit_solution(4604374302494779654)
XLA Ops:
  0.0 13.9 %shard_map.46 = bf16[128,512]{1,0:T(8,128)(2,1)S(1)} custom-call(bf16[128,512]{1,0:T(8,128)(2,1)} %q_hbm.1, bf16[128,128]{1,0:T(8,128)(2,1)} %k_hbm.1, bf16[128,128]{1,0:T(8,128)(2,1)} %v_hbm.1, s32[1,128]{1,0:T(1,128)} %bitcast.1), custom_call_target="tpu_custom_call" | custom-call | tf_op jit(solution)/shard_map/pallas_call | solution.py:216
  13.9 0.7 %copy.6 = bf16[128,512]{1,0:T(8,128)(2,1)} copy(bf16[128,512]{1,0:T(8,128)(2,1)S(1)} %shard_map.46) | data formatting | bytes 262144

commit v3 on v2

--- a/solution.py
+++ b/solution.py
@@ -11,6 +11,7 @@
 HEAD_WIDTH = 64
 NEG_FILL = -1e30
 MESH = pl.DeviceIdType.MESH
+PIECES = 2
 
 
 def kernel(n, inner, q_hbm, k_hbm, v_hbm, s_hbm, o_ref, qv, kbuf, vbuf, sbuf, qm, run_max, acc,
@@ -26,7 +27,15 @@
     z = me // inner
     x = me % inner
     partner = z * inner + (inner - 1 - x)
-    bufs = (sbuf, kbuf, vbuf)
+    kinds = 1 + 2 * PIECES
+    size = rows // PIECES
+
+    def piece(kind, block):
+        if kind == 0:
+            return sbuf.at[block]
+        buf = kbuf if kind <= PIECES else vbuf
+        return buf.at[block, pl.ds((kind - 1) % PIECES * size, size)]
+
 
     loads = [
         pltpu.make_async_copy(src, dst, in_sem.at[i])
@@ -51,25 +60,26 @@
     def onward(kind, row):
         block = row * inner + x
         return pltpu.make_async_remote_copy(
-            src_ref=bufs[kind].at[block], dst_ref=bufs[kind].at[block],
+            src_ref=piece(kind, block), dst_ref=piece(kind, block),
             send_sem=col_sem.at[kind, row], recv_sem=recv_sem.at[kind, block],
             device_id={"seq": me + inner}, device_id_type=MESH)
 
     def across(kind, row):
         block = row * inner + x
         return pltpu.make_async_remote_copy(
-            src_ref=bufs[kind].at[block], dst_ref=bufs[kind].at[block],
+            src_ref=piece(kind, block), dst_ref=piece(kind, block),
             send_sem=row_sem.at[kind, row], recv_sem=recv_sem.at[kind, block],
             device_id={"seq": partner}, device_id_type=MESH)
 
     def arrival(kind, block):
         return pltpu.make_async_remote_copy(
-            src_ref=bufs[kind].at[block], dst_ref=bufs[kind].at[block],
+            src_ref=piece(kind, block), dst_ref=piece(kind, block),
             send_sem=in_sem.at[0], recv_sem=recv_sem.at[kind, block],
             device_id={"seq": partner}, device_id_type=MESH)
 
-    for kind in range(3):
-        loads[kind].wait()
+    for kind in range(kinds):
+        if kind in (0, 1, 1 + PIECES):
+            loads[(0, 1, 1 + PIECES).index(kind)].wait()
 
         @pl.when(z < outer - 1)
         def _():
@@ -137,7 +147,7 @@
 
     def take(i, c):
         row = z - 1 - i
-        for kind in range(3):
+        for kind in range(kinds):
             arrival(kind, row * inner + x).wait_recv()
 
             @pl.when(z < outer - 1)
@@ -155,7 +165,7 @@
     if inner == 2:
         @pl.when(x == 1)
         def _():
-            for kind in range(3):
+            for kind in range(kinds):
                 arrival(kind, partner).wait_recv()
             attend(kbuf[partner], vbuf[partner], seen(sbuf[partner]), False)
 
@@ -164,7 +174,7 @@
     def step(i, c):
         row = z - 1 - i
         if inner == 2:
-            for kind in range(3):
+            for kind in range(kinds):
                 arrival(kind, row * inner + 1 - x).wait_recv()
         first = row * inner
         kk = kbuf[pl.ds(first, inner)].reshape(inner * rows, width)
@@ -188,11 +198,11 @@
     if inner == 2:
         @pl.when(x == 0)
         def _():
-            for kind in range(3):
+            for kind in range(kinds):
                 across(kind, z).wait_send()
 
         def drain_row(row, c):
-            for kind in range(3):
+            for kind in range(kinds):
                 across(kind, row).wait_send()
             return c
 
@@ -201,7 +211,7 @@
     @pl.when(z < outer - 1)
     def _():
         def drain_column(row, c):
-            for kind in range(3):
+            for kind in range(kinds):
                 onward(kind, row).wait_send()
             return c
 
@@ -227,9 +237,9 @@
             pltpu.VMEM((groups, heads, rows, rows), jnp.float32),
             pltpu.VMEM((groups, heads, rows, width), jnp.float32),
             pltpu.SemaphoreType.DMA((4,)),
-            pltpu.SemaphoreType.DMA((3, n // inner)),
-            pltpu.SemaphoreType.DMA((3, n // inner)),
-            pltpu.SemaphoreType.DMA((3, n)),
+            pltpu.SemaphoreType.DMA((1 + 2 * PIECES, n // inner)),
+            pltpu.SemaphoreType.DMA((1 + 2 * PIECES, n // inner)),
+            pltpu.SemaphoreType.DMA((1 + 2 * PIECES, n)),
         ],
         compiler_params=pltpu.CompilerParams(collective_id=0, has_side_effects=True),
     )(queries, key_matrix, value_matrix, segment_ids.reshape(1, rows))

time: 14.7 us -> 14.5 us (0.986)
  Pallas kernels: 13.9 us -> 13.7 us
    pallas_call x1, Pallas kernels: 13.9 us -> 13.7 us  [per_device(): pl.pallas_call(functools.partial(kernel, n, inner), out_shape=pltpu.VMEM(...]
where the time goes in v3:
time: 14.5 us; the launch traced here: 14.3 us
  Pallas kernels  13.7 us (94%)
  local copies, waits for them, and re-layouts  0.66 us (5%)
    pallas_call x1, Pallas kernels, per_device(): pl.pallas_call(functools.partial(kernel, n, inner), out_shape=pltpu.VMEM(...  13.7 us
    unnamed x1, local copies, waits for them, and re-layouts  0.66 us

profile of v3, /device:TPU:28, one launch (start us, length us, event | category | flops | bytes accessed | tf_op | source)
XLA Modules:
  0.0 14.3 jit_solution(2230179412623526657)
XLA Ops:
  0.0 13.7 %shard_map.46 = bf16[128,512]{1,0:T(8,128)(2,1)S(1)} custom-call(bf16[128,512]{1,0:T(8,128)(2,1)} %q_hbm.1, bf16[128,128]{1,0:T(8,128)(2,1)} %k_hbm.1, bf16[128,128]{1,0:T(8,128)(2,1)} %v_hbm.1, s32[1,128]{1,0:T(1,128)} %bitcast.1), custom_call_target="tpu_custom_call" | custom-call | tf_op jit(solution)/shard_map/pallas_call | solution.py:226
  13.7 0.7 %copy.6 = bf16[128,512]{1,0:T(8,128)(2,1)} copy(bf16[128,512]{1,0:T(8,128)(2,1)S(1)} %shard_map.46) | data formatting | bytes 262144

commit v4 on v3

--- a/solution.py
+++ b/solution.py
@@ -104,13 +104,13 @@
 
     seg_q = jnp.transpose(jnp.broadcast_to(sbuf[me], (rows, rows)))
 
-    def attend(kk, vv, vis, first):
+    def attend(kk, load_values, vis, first):
+        vv = None
         count = kk.shape[0]
         bias = jnp.where(vis, 0.0, NEG_FILL).astype(jnp.float32)
         ones = jnp.ones((count, half), jnp.bfloat16)
         for g in range(groups):
             kg = kk[:, g * half:(g + 1) * half]
-            vg = vv[:, g * half:(g + 1) * half]
             kd = jnp.concatenate([kg, kg], axis=1)
             heads = 2 * per_group
             s = lax.dot_general(
@@ -125,6 +125,9 @@
                 new = jnp.maximum(old, top)
             run_max[g] = new
             p = jnp.exp(s - jnp.concatenate([new] * (count // rows), axis=-1)).astype(jnp.bfloat16)
+            if vv is None:
+                vv = load_values()
+            vg = vv[:, g * half:(g + 1) * half]
             sides = (jnp.concatenate([vg, ones], axis=1), jnp.concatenate([ones, vg], axis=1))
             for side in range(2):
                 part = slice(side * per_group, (side + 1) * per_group)
@@ -139,7 +142,7 @@
     row_at = lax.broadcasted_iota(jnp.int32, (rows, rows), 0)
     col_at = lax.broadcasted_iota(jnp.int32, (rows, rows), 1)
     seg_k = jnp.broadcast_to(sbuf[me], (rows, rows))
-    attend(kbuf[me], vbuf[me], (col_at <= row_at) & ((seg_k == seg_q) | (seg_k == 0)), True)
+    attend(kbuf[me], lambda: vbuf[me], (col_at <= row_at) & ((seg_k == seg_q) | (seg_k == 0)), True)
 
     def seen(seg):
         seg = jnp.broadcast_to(seg, (rows, rows))
@@ -162,26 +165,34 @@
     def _():
         take(0, 0)
 
+    lax.fori_loop(1, z, take, 0)
+
+    def values_of(block, first, count):
+        def load():
+            if inner == 2:
+                for kind in range(1 + PIECES, kinds):
+                    arrival(kind, block).wait_recv()
+            return vbuf[pl.ds(first, count)].reshape(count * rows, width)
+
+        return load
+
     if inner == 2:
         @pl.when(x == 1)
         def _():
-            for kind in range(kinds):
+            for kind in range(1 + PIECES):
                 arrival(kind, partner).wait_recv()
-            attend(kbuf[partner], vbuf[partner], seen(sbuf[partner]), False)
-
-    lax.fori_loop(1, z, take, 0)
+            attend(kbuf[partner], values_of(partner, partner, 1), seen(sbuf[partner]), False)
 
     def step(i, c):
         row = z - 1 - i
         if inner == 2:
-            for kind in range(kinds):
+            for kind in range(1 + PIECES):
                 arrival(kind, row * inner + 1 - x).wait_recv()
         first = row * inner
         kk = kbuf[pl.ds(first, inner)].reshape(inner * rows, width)
-        vv = vbuf[pl.ds(first, inner)].reshape(inner * rows, width)
         vis = jnp.concatenate(
             [jnp.where(seen(sbuf[first + i]), 1, 0) for i in range(inner)], axis=1) == 1
-        attend(kk, vv, vis, False)
+        attend(kk, values_of(first + 1 - x, first, inner), vis, False)
         return c
 
     lax.fori_loop(0, z, step, 0)

time: 14.5 us -> 14.4 us (level)
  the two profiles are of different devices: /device:TPU:28 before, /device:TPU:30 now
where the time goes in v4:
time: 14.4 us; the launch traced here: 14.3 us
  Pallas kernels  13.6 us (94%)
  local copies, waits for them, and re-layouts  0.66 us (5%)
    pallas_call x1, Pallas kernels, per_device(): pl.pallas_call(functools.partial(kernel, n, inner), out_shape=pltpu.VMEM(...  13.6 us
    unnamed x1, local copies, waits for them, and re-layouts  0.66 us

profile of v4, /device:TPU:30, one launch (start us, length us, event | category | flops | bytes accessed | tf_op | source)
XLA Modules:
  0.0 14.3 jit_solution(6352351584215046085)
XLA Ops:
  0.0 13.6 %shard_map.46 = bf16[128,512]{1,0:T(8,128)(2,1)S(1)} custom-call(bf16[128,512]{1,0:T(8,128)(2,1)} %q_hbm.1, bf16[128,128]{1,0:T(8,128)(2,1)} %k_hbm.1, bf16[128,128]{1,0:T(8,128)(2,1)} %v_hbm.1, s32[1,128]{1,0:T(1,128)} %bitcast.1), custom_call_target="tpu_custom_call" | custom-call | tf_op jit(solution)/shard_map/pallas_call | solution.py:237
  13.6 0.7 %copy.6 = bf16[128,512]{1,0:T(8,128)(2,1)} copy(bf16[128,512]{1,0:T(8,128)(2,1)S(1)} %shard_map.46) | data formatting | bytes 262144
